TPU v7x, 32 devices: a whole 2x2x4 slice. The times are simulated.
32 devices in a mesh: seq: 16 (over z, x, core), mp: 2 (over y).
Axes of the slice: x: 2, y: 2, z: 4, core: 2. Of those that a mesh axis runs over, the one named last changes fastest.
Arguments:
- x_inner: bfloat16 [2, 4096, 5120], P(None, 'seq', 'mp'), may hold values from -6 to 6
- z_gate: bfloat16 [2, 4096, 5120], P(None, 'seq', 'mp'), may hold values from -6 to 6
- b_input: bfloat16 [2, 4096, 128], P(None, 'seq'), may hold values from -6 to 6
- c_input: bfloat16 [2, 4096, 128], P(None, 'seq'), may hold values from -6 to 6
- dt_raw: float32 [2, 4096, 80], P(None, 'seq', 'mp'), may hold values from -3 to 3
- doc_ids: int32 [2, 4096], P(None, 'seq'), may hold values from 0 to 2, never falling along the last dimension, each value on 1 to 2048 neighbouring positions
- conv_x: bfloat16 [4, 5120], P(None, 'mp'), may hold values from -3 to 3
- conv_b: bfloat16 [4, 128], replicated, may hold values from -3 to 3
- conv_c: bfloat16 [4, 128], replicated, may hold values from -3 to 3
- dt_bias: float32 [80], P('mp'), as said below
- decay_rate: float32 [80], P('mp'), may hold values from 0.0625 to 0.25
- norm_gain: float32 [5120], P('mp'), may hold values from 0.25 to 1.75
- w_out: bfloat16 [5120, 2560], P('mp'), may hold values from -0.078125 to 0.078125
Outputs:
- layer_out: bfloat16 [2, 4096, 2560], P(None, 'seq', 'mp')
Inputs may be any that keep to these rules, and one draw needn't show every extreme that they name: `doc_ids`: in each sequence the document numbers start at 0, never fall and rise by one at each new document; there are three documents, the longest exactly 2048 positions. `dt_bias`: softplus of each entry lies between 8/4096 and 1.
All inputs are finite; a program needn't handle non-finite values.
Results may differ from a plain program's by a relative error of at most 0.02.
Values may be sent and summed in bfloat16 or wider, within the bound.
A program may use at most 128 MiB of HBM per device.

v0:
```python
import jax
import jax.numpy as jnp
from jax import lax
from jax.sharding import PartitionSpec as P

BLOCK = 256
INNER = 5120


EPSILON = 1e-05


def passed_along(value, axis, steps):
    count = lax.axis_size(axis)
    first, last = max(0, -steps), min(count, count - steps)
    return lax.ppermute(value, axis, [(source, source + steps) for source in range(first, last)])


def prefix_2(value, axis, join, neutral, backward):
    count, mine = lax.axis_size(axis), lax.axis_index(axis)
    pieces = jax.tree.map(lambda part: lax.all_gather(part, axis), value)
    if backward:
        pieces = jax.tree.map(lambda part: part[::-1], pieces)
        mine = count - 1 - mine
    total = jax.tree.map(
        lambda part, zero: jnp.full_like(part, 0) + jnp.asarray(zero, part.dtype), value, neutral
    )

    def lap(position, total):
        longer = join(total, jax.tree.map(lambda part: part[position], pieces))
        return jax.tree.map(lambda new, old: jnp.where(position < mine, new, old), longer, total)

    return lax.fori_loop(0, count - 1, lap, total)


def causal_conv(window, marks, weight, length):
    taps = weight.shape[0]
    current = marks[:, taps - 1 :]
    total = jnp.zeros((window.shape[0], length, window.shape[2]), jnp.float32)
    for offset in range(taps):
        same = (marks[:, offset : offset + length] == current)[:, :, None]
        term = window[:, offset : offset + length].astype(jnp.float32) * weight[offset].astype(
            jnp.float32
        )
        total = total + jnp.where(same, term, 0.0)
    return jax.nn.silu(total).astype(jnp.bfloat16)


def combine_states(earlier, later):
    return (earlier[0] * later[0], later[0][:, :, None, None] * earlier[1] + later[1])


def block_terms(xs, bs, cs, steps, logs, docs, before):
    width = docs.shape[1]
    order = jnp.arange(width)
    causal = order[:, None] >= order[None, :]
    masked = causal[None] & (docs[:, :, None] == docs[:, None, :])
    scores = jnp.einsum("btn,bsn->bts", cs, bs, preferred_element_type=jnp.float32)
    spread = jnp.where(masked[:, :, :, None], logs[:, :, None, :] - logs[:, None, :, :], 0.0)
    mixing = jnp.where(
        masked[:, :, :, None], scores[:, :, :, None] * jnp.exp(spread) * steps[:, None, :, :], 0.0
    ).astype(jnp.bfloat16)
    inner = jnp.einsum("btsh,bshp->bthp", mixing, xs, preferred_element_type=jnp.float32)
    keeps = (docs == docs[:, -1:])[:, :, None]
    weights = jnp.where(keeps, jnp.exp(logs[:, -1:, :] - logs) * steps, 0.0)
    loaded = (weights[:, :, :, None] * bs[:, :, None, :].astype(jnp.float32)).astype(jnp.bfloat16)
    fresh = jnp.einsum("bshp,bshn->bhpn", xs, loaded, preferred_element_type=jnp.float32)
    carried = docs == before[:, None]
    entry = jnp.where(carried[:, :, None], jnp.exp(logs), 0.0)
    return (inner, fresh, entry, entry[:, -1, :])


def front_work(xs, bs, cs, steps, docs, before, rates):
    pieces = []
    running = jnp.zeros((xs.shape[0], xs.shape[2], xs.shape[3], bs.shape[2]), jnp.float32)
    product = jnp.ones((xs.shape[0], xs.shape[2]), jnp.float32)
    prior = before
    for index in range(xs.shape[1] // BLOCK):
        lower = index * BLOCK
        upper = lower + BLOCK
        steps_here = steps[:, lower:upper]
        logs = jnp.cumsum(-(steps_here * rates), axis=1)
        docs_here = docs[:, lower:upper]
        inner, fresh, entry, gate = block_terms(
            xs[:, lower:upper],
            bs[:, lower:upper],
            cs[:, lower:upper],
            steps_here,
            logs,
            docs_here,
            prior,
        )
        pieces.append((inner, entry, running, product))
        running = gate[:, :, None, None] * running + fresh
        product = product * gate
        prior = docs_here[:, -1]
    return (pieces, product, running)


def back_work(pieces, incoming, cs):
    outputs = []
    for index, piece in enumerate(pieces):
        inner, entry, running, product = piece
        entering = (product[:, :, None, None] * incoming + running).astype(jnp.bfloat16)
        cs_here = cs[:, index * BLOCK : (index + 1) * BLOCK]
        outer = jnp.einsum("btn,bhpn->bthp", cs_here, entering, preferred_element_type=jnp.float32)
        outputs.append(inner + entry[:, :, :, None] * outer)
    return jnp.concatenate(outputs, axis=1)


def body(
    x_inner,
    z_gate,
    b_input,
    c_input,
    dt_raw,
    doc_ids,
    conv_x,
    conv_b,
    conv_c,
    dt_bias,
    decay_rate,
    norm_gain,
    w_out,
):
    batch, length, channels = x_inner.shape
    heads = dt_raw.shape[2]
    state_dim = b_input.shape[2]
    edge = conv_x.shape[0] - 1
    tail = jnp.concatenate(
        [x_inner[:, length - edge :], b_input[:, length - edge :], c_input[:, length - edge :]],
        axis=2,
    )
    tail_docs = doc_ids[:, length - edge :]
    packed = jnp.concatenate([tail, (tail_docs + 1).astype(jnp.bfloat16)[:, :, None]], axis=2)
    moved = passed_along(packed, "seq", 1)
    halo_rows = moved[:, :, :-1]
    halo_docs = moved[:, :, -1].astype(jnp.int32) - 1
    marks = jnp.concatenate([halo_docs, doc_ids], axis=1)
    x_conv = causal_conv(
        jnp.concatenate([halo_rows[:, :, :channels], x_inner], axis=1), marks, conv_x, length
    )
    b_conv = causal_conv(
        jnp.concatenate([halo_rows[:, :, channels : channels + state_dim], b_input], axis=1),
        marks,
        conv_b,
        length,
    )
    c_conv = causal_conv(
        jnp.concatenate([halo_rows[:, :, channels + state_dim :], c_input], axis=1),
        marks,
        conv_c,
        length,
    )
    steps = jax.nn.softplus(dt_raw + dt_bias)
    xs = x_conv.reshape(batch, length, heads, channels // heads)
    before = halo_docs[:, -1]
    pieces, product, running = front_work(xs, b_conv, c_conv, steps, doc_ids, before, decay_rate)
    identity = (jnp.ones_like(product), jnp.zeros_like(running))
    prefix = tuple(
        (
            part.astype(kind)
            for part, kind in zip(
                prefix_2(
                    (product.astype(jnp.bfloat16), running.astype(jnp.bfloat16)),
                    "seq",
                    combine_states,
                    identity,
                    False,
                ),
                (jnp.float32, jnp.float32),
            )
        )
    )
    mixed_y = back_work(pieces, prefix[1], c_conv)
    gated = mixed_y.reshape(batch, length, channels) * jax.nn.silu(z_gate.astype(jnp.float32))
    squares = lax.psum(jnp.sum(gated * gated, axis=2), "mp")
    scale = lax.rsqrt(squares / INNER + EPSILON)
    normed = (gated * scale[:, :, None] * norm_gain).astype(jnp.bfloat16)
    flat = normed.reshape(batch * length, channels)
    width_out = w_out.shape[1] // lax.axis_size("mp")

    def project():
        columns = w_out
        return lax.dot_general(
            columns, flat, (((0,), (1,)), ((), ())), preferred_element_type=jnp.float32
        )

    summed = lax.psum_scatter(
        project().astype(jnp.bfloat16), "mp", scatter_dimension=0, tiled=True
    ).astype(jnp.float32)
    return summed.T.reshape(batch, length, width_out).astype(jnp.bfloat16)


def solution(mesh):
    placed = (
        P(None, "seq", "mp"),
        P(None, "seq", "mp"),
        P(None, "seq", None),
        P(None, "seq", None),
        P(None, "seq", "mp"),
        P(None, "seq"),
        P(None, "mp"),
        P(),
        P(),
        P("mp"),
        P("mp"),
        P("mp"),
        P("mp", None),
    )
    return jax.shard_map(
        body, mesh=mesh, in_specs=placed, out_specs=P(None, "seq", "mp"), check_vma=False
    )
```

profile of v0, /device:TPU:10, one launch (start us, length us, event | category | flops | bytes accessed | tf_op | source)
XLA Modules:
  0.0 265.1 jit_solution(10532270768824945010)
XLA Ops:
  6.5 1.0 slice.124
  7.5 0.7 slice.125
  8.2 0.7 slice.126
  8.9 0.8 fusion.29
  9.8 1.9 collective-permute-start
  11.8 1.4 bitcast_convert_fusion.3
  13.2 1.0 convert_reduce_fusion.3
  14.2 1.0 negate_bitcast_fusion
  15.2 1.2 reduce-window.6
  16.9 0.9 slice_reduce_fusion.2
  17.8 3.0 %copy.63 = bf16[2,256,2560]{1,2,0:T(8,128)(2,1)S(1)} copy(bf16[2,256,2560]{2,1,0:T(8,128)(2,1)} %param.15) | data formatting | bytes 5242880 | tf_op args[0]
  21.1 1.6 copy.62
  23.1 1.0 fusion.31
  24.0 8.3 %multiply_convert_fusion.3 = bf16[2,256,2560]{1,2,0:T(8,128)(2,1)S(1)} fusion(bf16[2,256,2560]{1,2,0:T(8,128)(2,1)S(1)} %copy.63, bf16[2,3,2560]{1,2,0:T(8,128)(2,1)} %copy.62, f32[2560]{0:T(1024)S(1)} %get-tuple-element.120, f32[2560]{0:T(1024)S(1)} %get-tuple-element.121, f32[2560]{0:T(1024)S(1)} %get-tuple-element.119, f32[2560]{0:T(1024)S(1)} %get-tuple-element.118, ...), kind=kLoop, calls=%fused_computation.24 | loop fusion | flops 36700160 | bytes 5316096 | tf_op jit(solution)/shard_map/convert_element_type | solution.py:46
  32.3 1.5 copy-done.2
  33.8 5.6 %add_convert_fusion = bf16[2,40,64,128]{3,2,1,0:T(8,128)(2,1)} fusion(bf16[2,256,40,64]{1,3,2,0:T(8,128)(2,1)S(1)} %bitcast.89, f32[2,256,128]{2,1,0:T(8,128)S(1)} %get-tuple-element.132, f32[2,256,40]{1,2,0:T(8,128)S(1)} %get-tuple-element.136, f32[2,40]{1,0:T(2,128)S(1)} %multiply_reduce_fusion.1), kind=kOutput, calls=%fused_computation.34 | convolution fusion | flops 342097920 | bytes 4276544 | tf_op jit(solution)/shard_map/bshp,bshn->bhpn/dot_general | solution.py:67
  39.5 4.5 %copy.70 = bf16[2,256,2560]{1,2,0:T(8,128)(2,1)} copy(bf16[2,256,2560]{2,1,0:T(8,128)(2,1)} %param.16) | data formatting | bytes 5242880 | tf_op args[1]
  44.1 0.8 compare_and_fusion
  45.1 15.2 %all-gather = bf16[32,1,40]{2,1,0:T(2,128)(2,1)S(1)} all-gather(bf16[2,1,40]{2,1,0:T(2,128)(2,1)S(1)} %copy.69), channel_id=2, replica_groups=mesh['seq'=16,'mp'=2] {'seq'}, dimensions={0}, use_global_device_ids=true | all-gather | bytes 2720 | tf_op jit(solution)/shard_map/all_gather | solution.py:21
  60.3 0.3 multiply_convert_fusion.7
  60.6 0.2 fusion.33
  60.9 88.8 %all-gather.4.cloned.1.call-done = bf16[32,40,64,128]{3,2,1,0:T(8,128)(2,1)} async-done(((bf16[2,40,64,128]{3,2,1,0:T(8,128)(2,1)}), bf16[32,40,64,128]{3,2,1,0:T(8,128)(2,1)}) %all-gather.4.cloned.1.call-update) | async-done | bytes 20971536 | tf_op jit(solution)/shard_map/all_gather | solution.py:21
  149.6 34.3 %while.14 = (s32[]{:T(128)}, bf16[2,40,64,128]{3,2,1,0:T(8,128)(2,1)S(1)}, s32[]{:T(128)}, bf16[16,2,40]{2,1,0:T(2,128)(2,1)S(1)}, bf16[16,2,40,64,128]{4,3,2,1,0:T(8,128)(2,1)}, /*index=5*/s32[]{:T(128)}, s32[]{:T(128)}) while((s32[]{:T(128)}, bf16[2,40,64,128]{3,2,1,0:T(8,128)(2,1)S(1)}, s32[]{:T(128)}, ...), condition=%wide.region_3.4_spmd.clone, body=%wide.region_2.3_spmd.clone.sunk | while | flops 2621444 | bytes 3932745 | solution.py:33
  149.6 2.2 fusion.42
  151.9 2.3 fusion.42
  154.2 2.3 fusion.42
  156.5 2.3 fusion.42
  158.8 2.3 fusion.42
  161.1 2.3 fusion.42
  163.4 2.3 fusion.42
  165.6 2.3 fusion.42
  167.9 2.3 fusion.42
  170.2 2.3 fusion.42
  172.5 2.3 fusion.42
  174.8 2.3 fusion.42
  177.1 2.3 fusion.42
  179.4 2.3 fusion.42
  181.6 2.3 fusion.42
  183.9 0.8 fusion.22
  184.8 0.9 copy-done.3
  185.7 6.1 %bitcast_add_fusion.1 = f32[2,256,40,64]{1,3,2,0:T(8,128)S(1)} fusion(f32[2,256,40,64]{1,3,2,0:T(8,128)S(1)} %fusion.22, f32[2,256,40]{1,2,0:T(8,128)S(1)} %get-tuple-element.137, bf16[2,256,40,64]{1,3,2,0:T(8,128)(2,1)S(1)} %bitcast.90, f32[2,256,40]{1,2,0:T(8,128)S(1)} %get-tuple-element.135, f32[2,256,40]{1,2,0:T(8,128)S(1)} %bitcast_bitcast_fusion, ...), kind=kOutput, calls=%fused_computation.19 | convolution fusion | flops 705167360 | bytes 14008320 | tf_op jit(solution)/shard_map/btsh,bshp->bthp/dot_general | solution.py:63
  191.8 2.3 copy-done.1
  194.1 2.0 multiply_reduce_fusion
  196.1 5.1 %psum.7 = f32[2,256]{1,0:T(2,128)S(1)} all-reduce(f32[2,256]{1,0:T(2,128)S(1)} %multiply_reduce_fusion), channel_id=1, replica_groups=mesh['seq'=16,'mp'=2] {'mp'}, use_global_device_ids=true, to_apply=%region_5.6 | all-reduce | flops 512 | bytes 4096 | tf_op jit(solution)/shard_map/psum | solution.py:177
  201.2 5.0 %multiply_convert_fusion.2 = bf16[2,256,2560]{1,2,0:T(8,128)(2,1)} fusion(f32[2560]{0:T(1024)S(1)} %copy-done.8, f32[2,256]{1,0:T(2,128)S(1)} %add_rsqrt_fusion, bf16[2,256,2560]{1,2,0:T(8,128)(2,1)S(1)} %copy-done, f32[2,256,40,64]{1,3,2,0:T(8,128)} %copy-done.1), kind=kLoop, calls=%fused_computation.20 | loop fusion | flops 11796480 | bytes 10498048 | tf_op jit(solution)/shard_map/convert_element_type | solution.py:179
  206.2 3.0 %copy.71 = bf16[2,256,2560]{2,1,0:T(8,128)(2,1)S(1)} copy(bf16[2,256,2560]{1,2,0:T(8,128)(2,1)} %multiply_convert_fusion.2) | data formatting | bytes 5242880 | tf_op jit(solution)/shard_map/convert_element_type | solution.py:179
  209.2 11.1 %fusion.15 = bf16[2560,512]{0,1:T(8,128)(2,1)} fusion(bf16[512,2560]{1,0:T(8,128)(2,1)S(1)} %bitcast.91, bf16[2560,2560]{1,0:T(8,128)(2,1)} %param.27), kind=kOutput, calls=%fused_computation.30 | convolution fusion | flops 6712197120 | bytes 18350080 | tf_op jit(solution)/shard_map/dot_general | solution.py:185
  220.3 38.0 %reduce-scatter.2.cloned.1.call-done = bf16[1280,512]{0,1:T(8,128)(2,1)} async-done(((bf16[2560,512]{0,1:T(8,128)(2,1)}), bf16[1280,512]{0,1:T(8,128)(2,1)}) %reduce-scatter.2.cloned.1.call-update) | async-done | bytes 1310736 | tf_op jit(solution)/shard_map/reduce_scatter | solution.py:189
  (66 shorter events, 1.8 us)
Async XLA Ops:
  6.5 16.5 %copy-start.5 = (bf16[2,256,128]{2,1,0:T(8,128)(2,1)S(1)}, bf16[2,256,128]{2,1,0:T(8,128)(2,1)}, u32[]{:S(2)}) copy-start(bf16[2,256,128]{2,1,0:T(8,128)(2,1)} %param.17) | copy-start | bytes 393220
  6.5 16.2 %copy-start.7 = (s32[2,256]{1,0:T(2,128)S(1)}, s32[2,256]{1,0:T(2,128)}, u32[]{:S(2)}) copy-start(s32[2,256]{1,0:T(2,128)} %param.20) | copy-start | bytes 6148
  6.5 143.1 %all-gather.4.cloned.1.call-start = ((), (), s32[]{:S(2)}) async-start(), calls=%async_computation.2 | async-start | bytes 22282240 | tf_op jit(solution)/shard_map/all_gather | solution.py:21
  9.8 10.9 %collective-permute-start = (bf16[2,3,2817]{2,0,1:T(2,128)(2,1)S(1)}, bf16[2,3,2817]{2,0,1:T(2,128)(2,1)S(1)}, u32[]{:S(2)}, u32[]{:S(2)}) collective-permute-start(bf16[2,3,2817]{2,0,1:T(2,128)(2,1)S(1)} %pad_maximum_fusion.3), channel_id=1, source_target_pairs={{0,2},{2,4},{4,6},{6,8},{8,10},{10,12},{12,14},{14,16},{16,18},{18... | collective-permute-start | bytes 101420 | tf_op jit(solution)/shard_map/ppermute | solution.py:16
  32.3 1.5 copy-start.2
  39.5 4.6 %copy-start.9 = (bf16[4,128]{1,0:T(4,128)(2,1)S(1)}, bf16[4,128]{1,0:T(4,128)(2,1)}, u32[]{:S(2)}) copy-start(bf16[4,128]{1,0:T(4,128)(2,1)} %param.23) | copy-start | bytes 3076
  39.5 20.9 %copy-start.4 = (bf16[2,256,128]{2,1,0:T(8,128)(2,1)S(1)}, bf16[2,256,128]{2,1,0:T(8,128)(2,1)}, u32[]{:S(2)}) copy-start(bf16[2,256,128]{2,1,0:T(8,128)(2,1)} %param.18) | copy-start | bytes 393220
  39.5 218.8 %reduce-scatter.2.cloned.1.call-start = ((), (), s32[]{:S(2)}) async-start(), calls=%async_computation.1 | async-start | bytes 3932160 | tf_op jit(solution)/shard_map/reduce_scatter | solution.py:189
  183.9 1.7 copy-start.3
  183.9 1.7 copy-start.6
  185.6 8.5 %copy-start = (bf16[2,256,2560]{1,2,0:T(8,128)(2,1)S(1)}, bf16[2,256,2560]{1,2,0:T(8,128)(2,1)}, u32[]{:S(2)}) copy-start(bf16[2,256,2560]{1,2,0:T(8,128)(2,1)} %copy.70) | copy-start | bytes 7864324
  191.8 2.3 copy-start.1
  194.1 7.1 %copy-start.8 = (f32[2560]{0:T(1024)S(1)}, f32[2560]{0:T(1024)}, u32[]{:S(2)}) copy-start(f32[2560]{0:T(1024)} %param.26) | copy-start | bytes 30724
Sparse Core Ops, SparseCore 0:
  39.6 109.9 all-gather.3
  220.4 37.8 reduce-scatter.1
where the time goes:
time: 268 us; the launch traced here: 265 us
  waiting for transfers between devices  127 us (47%)
  other arithmetic  57 us (21%)
  matrix products  23.9 us (9%)
  local copies, waits for them, and re-layouts  21 us (8%)
  blocking collectives  20.4 us (8%)
  between operations  13.7 us (5%)
    all_gather x1, waiting for transfers between devices, prefix_2(): pieces = jax.tree.map(lambda part: lax.all_gather(part, axis), value)  88.8 us
    reduce_scatter x1, waiting for transfers between devices, body(): lax.psum_scatter(project().astype(jnp.bfloat16), 'mp', scatter_dimension=...  38 us
    select_n x15, other arithmetic, lap(): jnp.where(position < mine, new, old)  33.8 us
    all_gather x1, blocking collectives, prefix_2(): pieces = jax.tree.map(lambda part: lax.all_gather(part, axis), value)  15.2 us
    unnamed x27, local copies, waits for them, and re-layouts  12.3 us
    dot_general x1, matrix products, project(): lax.dot_general(columns, flat, (((0,), (1,)), ((), ())), preferred_elemen...  11.1 us
    convert_element_type x2, other arithmetic, causal_conv(): return jax.nn.silu(total).astype(jnp.bfloat16)  8.55 us
    dot_general x1, matrix products, block_terms(): jnp.einsum('btsh,bshp->bthp', mixing, xs, preferred_element_type=jnp.floa...  6.13 us
  transfers between devices with their start and end apart: 3, of which 2 were waited for; matrix products, arithmetic and copies ran while one was open for 6% of the time, Pallas kernels for 0%

commit v1 on v0

v1 whole, which is shorter than its diff:
```python
import functools

import jax
import jax.numpy as jnp
from jax import lax
from jax.experimental import pallas as pl
from jax.experimental.pallas import tpu as pltpu
from jax.sharding import PartitionSpec as P

EPSILON = 1e-05
LANES = 128
EDGE = 16
LOG2E = 1.4426950408889634
CAP = 80.0
MESH = pl.DeviceIdType.MESH
F32 = jnp.float32
BF16 = jnp.bfloat16


def silu(value):
    half = 0.5 * value
    return half + half * jnp.tanh(half)


def wide(value, width):
    return value if width == LANES else jnp.concatenate([value] * (width // LANES), axis=1)


def kernel(
    dims,
    x_ref,
    z_hbm,
    b_ref,
    c_ref,
    dt_ref,
    doc_ref,
    wx_ref,
    wb_ref,
    wc_ref,
    bias_ref,
    rate_ref,
    gain_ref,
    w_hbm,
    out_ref,
    z_ref,
    w_ref,
    hx_ref,
    hb_ref,
    hc_ref,
    hd_ref,
    same_ref,
    xc_ref,
    cc_ref,
    bt_ref,
    score_ref,
    col_ref,
    load_ref,
    entry_ref,
    row_ref,
    pad_ref,
    s_ref,
    r_ref,
    g_ref,
    gr_ref,
    e_ref,
    o_ref,
    t_ref,
    en_ref,
    inner_ref,
    gn_ref,
    p_ref,
    q_ref,
    own_ref,
    sq_ref,
    sqr_ref,
    z_sem,
    w_sem,
    halo_send,
    halo_recv,
    s_send,
    s_recv,
    g_send,
    g_recv,
    e_send,
    e_recv,
    t_send,
    t_recv,
    p_send,
    p_recv,
    sq_send,
    sq_recv,
):
    batch, length, channels, heads, width, piece, aligned, n_mp = dims
    inner_total = channels * n_mp
    head_dim = channels // heads
    cw = 2 * LANES if channels % (2 * LANES) == 0 else LANES
    per_tile = LANES // head_dim
    per_chunk = cw // head_dim
    chunks = channels // cw
    units = batch * chunks
    steps = units // 2
    pieces = width // piece
    n_seq = lax.axis_size("seq")
    me = lax.axis_index("seq")
    my = lax.axis_index("mp")
    core = lax.rem(me, 2)
    sibling = me + 1 - 2 * core

    def blocks(k):
        if aligned:
            return w_hbm.at[:, pl.ds(pl.multiple_of(k * piece, piece), piece)]
        return w_hbm.at[k]

    barrier = pltpu.get_barrier_semaphore()
    expected = jnp.int32(n_mp - 1)
    for distance in (-2, -1, 1, 2):
        there = me + distance
        valid = jnp.logical_and(there >= 0, there < n_seq)
        expected = expected + valid.astype(jnp.int32)

        @pl.when(valid)
        def _(there=there):
            pl.semaphore_signal(barrier, inc=1, device_id={"seq": there}, device_id_type=MESH)

    for r in range(1, n_mp):
        pl.semaphore_signal(
            barrier, inc=1, device_id={"mp": lax.rem(my + r, n_mp)}, device_id_type=MESH
        )
    z_copy = pltpu.make_async_copy(z_hbm, z_ref, z_sem)
    z_copy.start()

    def w_copy(k):
        return pltpu.make_async_copy(blocks(k), w_ref.at[k], w_sem.at[k])

    def w_start(k, _):
        w_copy(k).start()
        return 0

    pl.semaphore_wait(barrier, expected)

    def remote(src, dst, send, recv, **there):
        return pltpu.make_async_remote_copy(
            src_ref=src,
            dst_ref=dst,
            send_sem=send,
            recv_sem=recv,
            device_id=there,
            device_id_type=MESH,
        )

    right = lax.rem(me + 1, n_seq)
    last = pl.ds(length - EDGE, EDGE)
    halos = [
        remote(doc_ref, hd_ref, halo_send.at[0], halo_recv.at[0], seq=right),
        remote(b_ref.at[:, last], hb_ref, halo_send.at[1], halo_recv.at[1], seq=right),
        remote(c_ref.at[:, last], hc_ref, halo_send.at[2], halo_recv.at[2], seq=right),
        remote(x_ref.at[:, last], hx_ref, halo_send.at[3], halo_recv.at[3], seq=right),
    ]

    @pl.when(me < n_seq - 1)
    def _():
        for halo in halos:
            halo.start()

    lax.fori_loop(0, n_mp * pieces, w_start, 0)

    @pl.when(me == 0)
    def _():
        hd_ref[...] = jnp.full_like(hd_ref, -1.0)
        hb_ref[...] = jnp.zeros_like(hb_ref)
        hc_ref[...] = jnp.zeros_like(hc_ref)
        hx_ref[...] = jnp.zeros_like(hx_ref)

    @pl.when(me < 2)
    def _():
        e_ref[...] = jnp.zeros_like(e_ref)

    rows = lax.broadcasted_iota(jnp.int32, (length, length), 0)
    columns = lax.broadcasted_iota(jnp.int32, (length, length), 1)
    causal = rows >= columns
    triangle = jnp.where(causal, 1.0, 0.0).astype(F32)
    lane_ids = lax.broadcasted_iota(jnp.int32, (length, LANES), 1)

    for b in range(batch):
        step = dt_ref[b] + bias_ref[...]
        step = jnp.maximum(step, 0.0) + jnp.log1p(jnp.exp(-jnp.abs(step)))
        pad_ref[b] = jnp.zeros((length, LANES), F32)
        pad_ref[batch + b] = jnp.ones((length, LANES), F32)
        pad_ref[b, :, 0:heads] = -(step * rate_ref[...])
        pad_ref[batch + b, :, 0:heads] = step
        logs = jnp.dot(
            triangle, pad_ref[b], precision=lax.Precision.HIGHEST, preferred_element_type=F32
        )
        col_ref[b] = logs * LOG2E
        row_ref[b] = (logs * LOG2E - jnp.log(pad_ref[batch + b]) * LOG2E).T

    @pl.when(me > 0)
    def _():
        for halo in halos:
            halo.wait_recv()

    def conv(now, halo, weight, same):
        full = jnp.concatenate([halo.astype(F32), now.astype(F32)], axis=0)
        taps = weight.shape[0]
        weight = weight.astype(F32)
        total = full[EDGE:] * weight[taps - 1 : taps]
        for lag in range(1, taps):
            shifted = pltpu.roll(full, lag, 0)[EDGE:]
            total = total + shifted * same[lag - 1] * weight[taps - 1 - lag : taps - lag]
        return silu(total)

    for b in range(batch):
        doc_row = doc_ref[b, 0:1, :]
        doc_col = jnp.broadcast_to(doc_row, (LANES, length)).T
        old_col = jnp.broadcast_to(hd_ref[b, 0:1, :], (LANES, length)).T
        full = jnp.concatenate([old_col[length - EDGE :], doc_col], axis=0)
        for lag in range(1, wx_ref.shape[0]):
            mark = pltpu.roll(full, lag, 0)[EDGE:]
            same = jnp.where(mark == doc_col, 1.0, 0.0).astype(F32)
            same_ref[b, lag - 1] = wide(same, cw)
        sames = [same_ref[b, lag, :, 0:LANES] for lag in range(wx_ref.shape[0] - 1)]
        b_conv = conv(b_ref[b], hb_ref[b], wb_ref[...], sames).astype(BF16)
        c_conv = conv(c_ref[b], hc_ref[b], wc_ref[...], sames).astype(BF16)
        cc_ref[b] = c_conv
        bt = b_conv.astype(F32).T.astype(BF16)
        bt_ref[b] = bt
        scores = jnp.dot(c_conv, bt, preferred_element_type=F32)
        masked = jnp.logical_and(causal, wide(doc_col, length) == doc_row)
        score_ref[b] = jnp.where(masked, scores, 0.0)
        logs = col_ref[b]
        step = pad_ref[batch + b]
        keeps = doc_col == doc_col[length - 1 : length]
        load_ref[b] = jnp.where(keeps, jnp.exp2(logs[length - 1 : length] - logs) * step, 0.0)
        before = old_col[length - 1 : length]
        entry_ref[b] = jnp.where(doc_col == before, jnp.exp2(logs), 0.0)

    def place(u):
        b = u // chunks
        c = u - b * chunks
        return b, c, pl.ds(pl.multiple_of(c * cw, cw), cw)

    def turned(value, c):
        return pltpu.roll(value, lax.rem(LANES - c * per_chunk, LANES), 1)

    def expand(value):
        ids = lax.broadcasted_iota(jnp.int32, (value.shape[0], LANES), 1)
        parts = []
        for tile in range(cw // LANES):
            first = tile * per_tile
            part = value[:, first : first + 1]
            for more in range(1, per_tile):
                column = value[:, first + more : first + more + 1]
                part = jnp.where(ids < more * head_dim, part, column)
            parts.append(jnp.broadcast_to(part, (value.shape[0], LANES)))
        return jnp.concatenate(parts, axis=1) if len(parts) > 1 else parts[0]

    def s_copy(u):
        return remote(
            s_ref.at[u], r_ref.at[u // 2], s_send.at[u // 2], s_recv.at[u // 2], seq=sibling
        )

    def front(u, _):
        b, c, where = place(u)
        sames = [same_ref[b, lag] for lag in range(wx_ref.shape[0] - 1)]
        x_conv = conv(x_ref[b, :, where], hx_ref[b, :, where], wx_ref[:, where], sames)
        x_conv = x_conv.astype(BF16)
        xc_ref[b, :, where] = x_conv
        weights = expand(turned(load_ref[b], c))
        weighted = (x_conv.astype(F32) * weights).astype(BF16)
        s_ref[u] = jnp.dot(bt_ref[b], weighted, preferred_element_type=F32).astype(BF16)
        gate = expand(turned(entry_ref[b, length - 8 : length, :], c))
        g_ref[u] = jnp.broadcast_to(gate[7:8], (8, cw))

        @pl.when(lax.rem(u, 2) != core)
        def _():
            s_copy(u).start()

        return 0

    lax.fori_loop(0, units, front, 0)
    g_copy = remote(g_ref, gr_ref, g_send, g_recv, seq=sibling)
    g_copy.start()
    g_copy.wait_recv()
    ahead = lax.rem(me + 2, n_seq)

    def e_copy(i):
        return remote(o_ref.at[i], e_ref.at[i], e_send.at[i], e_recv.at[i], seq=ahead)

    def t_copy(i, owner):
        u = 2 * i + owner
        return remote(t_ref.at[i], en_ref.at[u], t_send.at[i], t_recv.at[i], seq=sibling)

    def inner_unit(u):
        b, c, where = place(u)
        turned_logs = turned(col_ref[b], c)
        scores = score_ref[b]
        for tile in range(cw // LANES):
            lanes = pl.ds(pl.multiple_of(c * cw + tile * LANES, LANES), LANES)
            xs = xc_ref[b, :, lanes]
            total = None
            for more in range(per_tile):
                head = tile * per_tile + more
                column = turned_logs[:, head : head + 1]
                row = row_ref[b, pl.ds(c * per_chunk + head, 1), :]
                mixing = scores * jnp.exp2(jnp.minimum(column - row, CAP))
                one = jnp.dot(mixing.astype(BF16), xs, preferred_element_type=F32)
                total = one if more == 0 else jnp.where(lane_ids < more * head_dim, total, one)
            inner_ref[b, :, lanes] = total

    def chain(i, _):
        u = 2 * i + core
        s_copy(2 * i).wait_recv()
        mine, theirs = s_ref[u].astype(F32), r_ref[i].astype(F32)
        my_gate, their_gate = g_ref[u, 0:1, :], gr_ref[u, 0:1, :]
        first = core == 0
        state_a = jnp.where(first, mine, theirs)
        state_b = jnp.where(first, theirs, mine)
        gate_a = jnp.where(first, my_gate, their_gate)
        gate_b = jnp.where(first, their_gate, my_gate)

        @pl.when(me >= 2)
        def _():
            e_copy(i).wait_recv()

        entering = e_ref[i].astype(F32)
        middle = gate_a * entering + state_a
        o_ref[i] = (gate_b * middle + state_b).astype(BF16)

        @pl.when(me + 2 < n_seq)
        def _():
            e_copy(i).start()

        t_ref[i] = jnp.where(first, middle, entering).astype(BF16)
        t_copy(i, core).start()
        en_ref[u] = jnp.where(first, entering, middle).astype(BF16)
        inner_unit(2 * i)
        inner_unit(2 * i + 1)
        return 0

    def t_wait(i, _):
        t_copy(i, 1 - core).wait_recv()
        return 0

    def p_slot(b, r, p):
        return (b * (n_mp - 1) + r - 1) * pieces + p

    def p_copy(b, r, p):
        slot = p_slot(b, r, p)
        return remote(
            p_ref.at[slot],
            q_ref.at[slot],
            p_send.at[slot],
            p_recv.at[slot],
            mp=lax.rem(my + r, n_mp),
        )

    def sq_copy(b, r):
        slot = b * (n_mp - 1) + r - 1
        return remote(
            sq_ref.at[b],
            sqr_ref.at[slot],
            sq_send.at[slot],
            sq_recv.at[slot],
            mp=lax.rem(my + r, n_mp),
        )

    def tail(b):
        def gate_unit(c, squares):
            where = pl.ds(pl.multiple_of(c * cw, cw), cw)
            outer = jnp.dot(cc_ref[b], en_ref[b * chunks + c], preferred_element_type=F32)
            mixed = inner_ref[b, :, where] + expand(turned(entry_ref[b], c)) * outer
            gated = mixed * silu(z_ref[b, :, where].astype(F32))
            gn_ref[:, where] = (gated * gain_ref[0:1, where]).astype(BF16)
            square = gated * gated
            for tile in range(cw // LANES):
                squares = squares + square[:, tile * LANES : (tile + 1) * LANES]
            return squares

        squares = lax.fori_loop(0, chunks, gate_unit, jnp.zeros((length, LANES), F32))
        sq_ref[b] = jnp.broadcast_to(jnp.sum(squares.T, axis=0, keepdims=True), (8, length))
        for r in range(1, n_mp):

            def project(p, _, r=r):
                k = lax.rem(my + r, n_mp) * pieces + p
                value = jnp.dot(gn_ref[...], w_ref[k], preferred_element_type=F32)
                p_ref[p_slot(b, r, p)] = value.astype(BF16)
                p_copy(b, r, p).start()
                return 0

            sq_copy(b, r).start()
            lax.fori_loop(0, pieces, project, 0)

        def project_own(p, _):
            value = jnp.dot(gn_ref[...], w_ref[my * pieces + p], preferred_element_type=F32)
            own_ref[b * pieces + p] = value
            return 0

        lax.fori_loop(0, pieces, project_own, 0)

    def finish(b):
        total = sq_ref[b]
        for r in range(1, n_mp):
            sq_copy(b, r).wait_recv()
            total = total + sqr_ref[b * (n_mp - 1) + r - 1]
        scale = lax.rsqrt(total[0:1] / inner_total + EPSILON)
        scale = jnp.broadcast_to(scale, (LANES, length)).T[:, 0:1]
        for p in range(pieces):
            value = own_ref[b * pieces + p]
            for r in range(1, n_mp):
                p_copy(b, r, p).wait_recv()
                value = value + q_ref[p_slot(b, r, p)].astype(F32)
            out_ref[b, :, p * piece : (p + 1) * piece] = (value * scale).astype(BF16)

    lower = 0
    for b in range(batch):
        upper = ((b + 1) * chunks + 1) // 2
        lax.fori_loop(lower, upper, chain, 0)
        lax.fori_loop(lower, upper, t_wait, 0)
        if b == 0:
            z_copy.wait()
            lax.fori_loop(0, n_mp * pieces, lambda k, _: (w_copy(k).wait(), 0)[1], 0)
        tail(b)
        lower = upper
    for b in range(batch):
        finish(b)

    @pl.when(me < n_seq - 1)
    def _():
        for halo in halos:
            halo.wait_send()

    g_copy.wait_send()

    def drain(i, _):
        s_copy(2 * i).wait_send()
        t_copy(i, core).wait_send()

        @pl.when(me + 2 < n_seq)
        def _():
            e_copy(i).wait_send()

        return 0

    lax.fori_loop(0, steps, drain, 0)
    for b in range(batch):
        for r in range(1, n_mp):
            sq_copy(b, r).wait_send()
            lax.fori_loop(0, pieces, lambda p, _, b=b, r=r: (p_copy(b, r, p).wait_send(), 0)[1], 0)


def body(
    x_inner,
    z_gate,
    b_input,
    c_input,
    dt_raw,
    doc_ids,
    conv_x,
    conv_b,
    conv_c,
    dt_bias,
    decay_rate,
    norm_gain,
    w_out,
):
    batch, length, channels = x_inner.shape
    heads = dt_raw.shape[2]
    n_state = b_input.shape[2]
    taps = conv_x.shape[0]
    n_mp = lax.axis_size("mp")
    width = w_out.shape[1] // n_mp
    aligned = width % LANES == 0
    piece = 2 * LANES if width % (2 * LANES) == 0 else width
    pieces = width // piece
    cw = 2 * LANES if channels % (2 * LANES) == 0 else LANES
    units = batch * channels // cw
    steps = units // 2
    weights = w_out
    if not aligned:
        weights = w_out.reshape(channels, n_mp, width).transpose(1, 0, 2)
    docs = jnp.broadcast_to(doc_ids.astype(F32)[:, None, :], (batch, 8, length))
    others = n_mp - 1
    dims = (batch, length, channels, heads, width, piece, aligned, n_mp)
    vmem = pl.BlockSpec(memory_space=pltpu.VMEM)
    hbm = pl.BlockSpec(memory_space=pl.ANY)
    dma = pltpu.SemaphoreType.DMA
    V = pltpu.VMEM
    return pl.pallas_call(
        functools.partial(kernel, dims),
        out_shape=jax.ShapeDtypeStruct((batch, length, width), BF16),
        in_specs=[vmem, hbm, vmem, vmem, vmem, vmem, vmem, vmem, vmem, vmem, vmem, vmem, hbm],
        out_specs=vmem,
        scratch_shapes=[
            V((batch, length, channels), BF16),
            V((n_mp * pieces, channels, piece), BF16),
            V((batch, EDGE, channels), BF16),
            V((batch, EDGE, n_state), BF16),
            V((batch, EDGE, n_state), BF16),
            V((batch, 8, length), F32),
            V((batch, taps - 1, length, cw), F32),
            V((batch, length, channels), BF16),
            V((batch, length, n_state), BF16),
            V((batch, n_state, length), BF16),
            V((batch, length, length), F32),
            V((batch, length, LANES), F32),
            V((batch, length, LANES), F32),
            V((batch, length, LANES), F32),
            V((batch, LANES, length), F32),
            V((2 * batch, length, LANES), F32),
            V((units, n_state, cw), BF16),
            V((steps, n_state, cw), BF16),
            V((units, 8, cw), F32),
            V((units, 8, cw), F32),
            V((steps, n_state, cw), BF16),
            V((steps, n_state, cw), BF16),
            V((steps, n_state, cw), BF16),
            V((units, n_state, cw), BF16),
            V((batch, length, channels), F32),
            V((length, channels), BF16),
            V((batch * others * pieces, length, piece), BF16),
            V((batch * others * pieces, length, piece), BF16),
            V((batch * pieces, length, piece), F32),
            V((batch, 8, length), F32),
            V((batch * others, 8, length), F32),
            dma,
            dma((n_mp * pieces,)),
            dma((4,)),
            dma((4,)),
            dma((steps,)),
            dma((steps,)),
            dma,
            dma,
            dma((steps,)),
            dma((steps,)),
            dma((steps,)),
            dma((steps,)),
            dma((batch * others * pieces,)),
            dma((batch * others * pieces,)),
            dma((batch * others,)),
            dma((batch * others,)),
        ],
        compiler_params=pltpu.CompilerParams(
            collective_id=0, has_side_effects=True, vmem_limit_bytes=62 * 1024 * 1024
        ),
        name="mixer",
    )(
        x_inner,
        z_gate,
        b_input,
        c_input,
        dt_raw,
        docs,
        conv_x,
        conv_b,
        conv_c,
        dt_bias[None, :],
        decay_rate[None, :],
        norm_gain[None, :],
        weights,
    )


def solution(mesh):
    placed = (
        P(None, "seq", "mp"),
        P(None, "seq", "mp"),
        P(None, "seq", None),
        P(None, "seq", None),
        P(None, "seq", "mp"),
        P(None, "seq"),
        P(None, "mp"),
        P(),
        P(),
        P("mp"),
        P("mp"),
        P("mp"),
        P("mp", None),
    )
    return jax.shard_map(
        body, mesh=mesh, in_specs=placed, out_specs=P(None, "seq", "mp"), check_vma=False
    )
```

time: 268 us -> 93.5 us (0.35)
  the two profiles are of different devices: /device:TPU:10 before, /device:TPU:27 now
where the time goes in v1:
time: 93.5 us; the launch traced here: 93.2 us
  Pallas kernels  86.4 us (92%)
  local copies, waits for them, and re-layouts  6.09 us (7%)
    pallas_call x1, Pallas kernels, body(): pl.pallas_call(functools.partial(kernel, dims), out_shape=jax.ShapeDtypeS...  86.4 us
    unnamed x2, local copies, waits for them, and re-layouts  4.18 us

profile of v1, /device:TPU:27, one launch (start us, length us, event | category | flops | bytes accessed | tf_op | source)
XLA Modules:
  0.0 93.2 jit_solution(15016355694659174818)
XLA Ops:
  0.0 0.7 convert_element_type.3
  0.7 1.3 %broadcast_in_dim.18.gain_ref = f32[1,2560]{1,0:T(1,128)} reshape(f32[2560]{0:T(1024)} %param.24) | data formatting | bytes 20480 | tf_op jit(solution)/shard_map/broadcast_in_dim | solution.py:558
  2.0 0.6 broadcast_in_dim.15.doc_ref
  2.6 1.7 %copy.14.dt_ref = f32[2,256,40]{2,1,0:T(8,128)} copy(f32[2,256,40]{1,2,0:T(8,128)} %param.17) | data formatting | bytes 163840 | tf_op args[4]
  4.3 86.4 %mixer.1 = bf16[2,256,1280]{2,1,0:T(8,128)(2,1)} custom-call(bf16[2,256,2560]{2,1,0:T(8,128)(2,1)} %x_ref.1, bf16[2,256,2560]{2,1,0:T(8,128)(2,1)} %z_hbm.1, bf16[2,256,128]{2,1,0:T(8,128)(2,1)} %b_ref.1, bf16[2,256,128]{2,1,0:T(8,128)(2,1)} %c_ref.1, f32[2,256,40]{2,1,0:T(8,128)} %copy.14.dt_ref, f32[2,8,256]{2,1,0:T(8,128)} %broadcast_in_dim.15.doc_ref, ...), custom_call_target="tpu_custom_call" | custom-call | tf_op jit(solution)/shard_map/mixer/pallas_call | solution.py:488
  90.7 2.5 %copy.16 = bf16[2,256,1280]{2,1,0:T(8,128)(2,1)} copy(bf16[2,256,1280]{2,1,0:T(8,128)(2,1)} %mixer.1) | data formatting | bytes 2621440

commit v2 on v1

--- a/solution.py
+++ b/solution.py
@@ -28,7 +28,7 @@
 
 def kernel(
     dims,
-    x_ref,
+    x_hbm,
     z_hbm,
     b_ref,
     c_ref,
@@ -42,6 +42,7 @@
     gain_ref,
     w_hbm,
     out_ref,
+    x_ref,
     z_ref,
     w_ref,
     hx_ref,
@@ -67,14 +68,18 @@
     t_ref,
     en_ref,
     inner_ref,
+    factor_ref,
     gn_ref,
     p_ref,
     q_ref,
     own_ref,
     sq_ref,
     sqr_ref,
+    x_sem,
     z_sem,
     w_sem,
+    doc_send,
+    doc_recv,
     halo_send,
     halo_recv,
     s_send,
@@ -93,7 +98,7 @@
     batch, length, channels, heads, width, piece, aligned, n_mp = dims
     inner_total = channels * n_mp
     head_dim = channels // heads
-    cw = 2 * LANES if channels % (2 * LANES) == 0 else LANES
+    cw = LANES
     per_tile = LANES // head_dim
     per_chunk = cw // head_dim
     chunks = channels // cw
@@ -127,7 +132,11 @@
             barrier, inc=1, device_id={"mp": lax.rem(my + r, n_mp)}, device_id_type=MESH
         )
     z_copy = pltpu.make_async_copy(z_hbm, z_ref, z_sem)
-    z_copy.start()
+    x_copies = [
+        pltpu.make_async_copy(x_hbm.at[b], x_ref.at[b], x_sem.at[b]) for b in range(batch)
+    ]
+    for x_copy in x_copies:
+        x_copy.start()
 
     def w_copy(k):
         return pltpu.make_async_copy(blocks(k), w_ref.at[k], w_sem.at[k])
@@ -151,22 +160,28 @@
     right = lax.rem(me + 1, n_seq)
     last = pl.ds(length - EDGE, EDGE)
     halos = [
-        remote(doc_ref, hd_ref, halo_send.at[0], halo_recv.at[0], seq=right),
-        remote(b_ref.at[:, last], hb_ref, halo_send.at[1], halo_recv.at[1], seq=right),
-        remote(c_ref.at[:, last], hc_ref, halo_send.at[2], halo_recv.at[2], seq=right),
-        remote(x_ref.at[:, last], hx_ref, halo_send.at[3], halo_recv.at[3], seq=right),
+        [
+            remote(b_ref.at[b, last], hb_ref.at[b], halo_send.at[b, 0], halo_recv.at[b, 0], seq=right),
+            remote(c_ref.at[b, last], hc_ref.at[b], halo_send.at[b, 1], halo_recv.at[b, 1], seq=right),
+            remote(x_hbm.at[b, last], hx_ref.at[b], halo_send.at[b, 2], halo_recv.at[b, 2], seq=right),
+        ]
+        for b in range(batch)
     ]
+    doc_copy = remote(doc_ref, hd_ref, doc_send, doc_recv, seq=right)
 
     @pl.when(me < n_seq - 1)
     def _():
+        doc_copy.start()
         for halo in halos:
-            halo.start()
-
+            for copy in halo:
+                copy.start()
+
+    z_copy.start()
     lax.fori_loop(0, n_mp * pieces, w_start, 0)
 
     @pl.when(me == 0)
     def _():
-        hd_ref[...] = jnp.full_like(hd_ref, -1.0)
+        hd_ref[...] = jnp.full_like(hd_ref, -1)
         hb_ref[...] = jnp.zeros_like(hb_ref)
         hc_ref[...] = jnp.zeros_like(hc_ref)
         hx_ref[...] = jnp.zeros_like(hx_ref)
@@ -182,7 +197,9 @@
     lane_ids = lax.broadcasted_iota(jnp.int32, (length, LANES), 1)
 
     for b in range(batch):
-        step = dt_ref[b] + bias_ref[...]
+        row_ref[b] = jnp.zeros((LANES, length), F32)
+        row_ref[b, 0:heads, :] = dt_ref[b]
+        step = row_ref[b].T[:, 0:heads] + bias_ref[...]
         step = jnp.maximum(step, 0.0) + jnp.log1p(jnp.exp(-jnp.abs(step)))
         pad_ref[b] = jnp.zeros((length, LANES), F32)
         pad_ref[batch + b] = jnp.ones((length, LANES), F32)
@@ -196,8 +213,7 @@
 
     @pl.when(me > 0)
     def _():
-        for halo in halos:
-            halo.wait_recv()
+        doc_copy.wait_recv()
 
     def conv(now, halo, weight, same):
         full = jnp.concatenate([halo.astype(F32), now.astype(F32)], axis=0)
@@ -209,10 +225,17 @@
             total = total + shifted * same[lag - 1] * weight[taps - 1 - lag : taps - lag]
         return silu(total)
 
-    for b in range(batch):
-        doc_row = doc_ref[b, 0:1, :]
+    def prepare(b):
+        x_copies[b].wait()
+
+        @pl.when(me > 0)
+        def _():
+            for copy in halos[b]:
+                copy.wait_recv()
+
+        doc_row = doc_ref[b : b + 1, :].astype(F32)
         doc_col = jnp.broadcast_to(doc_row, (LANES, length)).T
-        old_col = jnp.broadcast_to(hd_ref[b, 0:1, :], (LANES, length)).T
+        old_col = jnp.broadcast_to(hd_ref[b : b + 1, :].astype(F32), (LANES, length)).T
         full = jnp.concatenate([old_col[length - EDGE :], doc_col], axis=0)
         for lag in range(1, wx_ref.shape[0]):
             mark = pltpu.roll(full, lag, 0)[EDGE:]
@@ -277,10 +300,23 @@
 
         return 0
 
-    lax.fori_loop(0, units, front, 0)
-    g_copy = remote(g_ref, gr_ref, g_send, g_recv, seq=sibling)
-    g_copy.start()
-    g_copy.wait_recv()
+    bounds = [((b * chunks + 1) // 2, ((b + 1) * chunks + 1) // 2) for b in range(batch)]
+
+    def g_copy(b):
+        lower, upper = bounds[b]
+        own = pl.ds(2 * lower, 2 * (upper - lower))
+        return remote(g_ref.at[own], gr_ref.at[own], g_send.at[b], g_recv.at[b], seq=sibling)
+
+    def fronts(b):
+        if chunks % 2 == 0:
+            prepare(b)
+        elif b == 0:
+            for every in range(batch):
+                prepare(every)
+        lower, upper = bounds[b]
+        lax.fori_loop(2 * lower, 2 * upper, front, 0)
+        g_copy(b).start()
+
     ahead = lax.rem(me + 2, n_seq)
 
     def e_copy(i):
@@ -290,7 +326,7 @@
         u = 2 * i + owner
         return remote(t_ref.at[i], en_ref.at[u], t_send.at[i], t_recv.at[i], seq=sibling)
 
-    def inner_unit(u):
+    def inner_unit(u, _):
         b, c, where = place(u)
         turned_logs = turned(col_ref[b], c)
         scores = score_ref[b]
@@ -305,7 +341,10 @@
                 mixing = scores * jnp.exp2(jnp.minimum(column - row, CAP))
                 one = jnp.dot(mixing.astype(BF16), xs, preferred_element_type=F32)
                 total = one if more == 0 else jnp.where(lane_ids < more * head_dim, total, one)
-            inner_ref[b, :, lanes] = total
+            opened = silu(z_ref[b, :, lanes].astype(F32))
+            inner_ref[b, :, lanes] = total * opened
+            factor_ref[b, :, lanes] = expand(turned(entry_ref[b], c)) * opened
+        return 0
 
     def chain(i, _):
         u = 2 * i + core
@@ -333,8 +372,6 @@
         t_ref[i] = jnp.where(first, middle, entering).astype(BF16)
         t_copy(i, core).start()
         en_ref[u] = jnp.where(first, entering, middle).astype(BF16)
-        inner_unit(2 * i)
-        inner_unit(2 * i + 1)
         return 0
 
     def t_wait(i, _):
@@ -368,9 +405,8 @@
         def gate_unit(c, squares):
             where = pl.ds(pl.multiple_of(c * cw, cw), cw)
             outer = jnp.dot(cc_ref[b], en_ref[b * chunks + c], preferred_element_type=F32)
-            mixed = inner_ref[b, :, where] + expand(turned(entry_ref[b], c)) * outer
-            gated = mixed * silu(z_ref[b, :, where].astype(F32))
-            gn_ref[:, where] = (gated * gain_ref[0:1, where]).astype(BF16)
+            gated = inner_ref[b, :, where] + factor_ref[b, :, where] * outer
+            gn_ref[:, where] = (gated * gain_ref[pl.ds(c, 1), :]).astype(BF16)
             square = gated * gated
             for tile in range(cw // LANES):
                 squares = squares + square[:, tile * LANES : (tile + 1) * LANES]
@@ -411,25 +447,60 @@
                 value = value + q_ref[p_slot(b, r, p)].astype(F32)
             out_ref[b, :, p * piece : (p + 1) * piece] = (value * scale).astype(BF16)
 
-    lower = 0
+    def inners():
+        z_copy.wait()
+        lax.fori_loop(0, units, inner_unit, 0)
+
+    def chains(b):
+        lower, upper = bounds[b]
+        g_copy(b).wait_recv()
+        lax.fori_loop(lower, upper, chain, 0)
+
+    def returns(b):
+        lower, upper = bounds[b]
+        lax.fori_loop(lower, upper, t_wait, 0)
+
+    late = me >= n_seq // 2
+    fronts(0)
+
+    @pl.when(late)
+    def _():
+        for b in range(1, batch):
+            fronts(b)
+        inners()
+
+    chains(0)
+
+    @pl.when(jnp.logical_not(late))
+    def _():
+        for b in range(1, batch):
+            fronts(b)
+        for b in range(1, batch):
+            chains(b)
+        inners()
+
+    lax.fori_loop(0, n_mp * pieces, lambda k, _: (w_copy(k).wait(), 0)[1], 0)
     for b in range(batch):
-        upper = ((b + 1) * chunks + 1) // 2
-        lax.fori_loop(lower, upper, chain, 0)
-        lax.fori_loop(lower, upper, t_wait, 0)
-        if b == 0:
-            z_copy.wait()
-            lax.fori_loop(0, n_mp * pieces, lambda k, _: (w_copy(k).wait(), 0)[1], 0)
+        if b > 0:
+
+            @pl.when(late)
+            def _(b=b):
+                chains(b)
+
+        returns(b)
         tail(b)
-        lower = upper
     for b in range(batch):
         finish(b)
 
     @pl.when(me < n_seq - 1)
     def _():
+        doc_copy.wait_send()
         for halo in halos:
-            halo.wait_send()
-
-    g_copy.wait_send()
+            for copy in halo:
+                copy.wait_send()
+
+    for b in range(batch):
+        g_copy(b).wait_send()
 
     def drain(i, _):
         s_copy(2 * i).wait_send()
@@ -472,13 +543,12 @@
     aligned = width % LANES == 0
     piece = 2 * LANES if width % (2 * LANES) == 0 else width
     pieces = width // piece
-    cw = 2 * LANES if channels % (2 * LANES) == 0 else LANES
+    cw = LANES
     units = batch * channels // cw
     steps = units // 2
     weights = w_out
     if not aligned:
         weights = w_out.reshape(channels, n_mp, width).transpose(1, 0, 2)
-    docs = jnp.broadcast_to(doc_ids.astype(F32)[:, None, :], (batch, 8, length))
     others = n_mp - 1
     dims = (batch, length, channels, heads, width, piece, aligned, n_mp)
     vmem = pl.BlockSpec(memory_space=pltpu.VMEM)
@@ -488,15 +558,16 @@
     return pl.pallas_call(
         functools.partial(kernel, dims),
         out_shape=jax.ShapeDtypeStruct((batch, length, width), BF16),
-        in_specs=[vmem, hbm, vmem, vmem, vmem, vmem, vmem, vmem, vmem, vmem, vmem, vmem, hbm],
+        in_specs=[hbm, hbm, vmem, vmem, vmem, vmem, vmem, vmem, vmem, vmem, vmem, vmem, hbm],
         out_specs=vmem,
         scratch_shapes=[
+            V((batch, length, channels), BF16),
             V((batch, length, channels), BF16),
             V((n_mp * pieces, channels, piece), BF16),
             V((batch, EDGE, channels), BF16),
             V((batch, EDGE, n_state), BF16),
             V((batch, EDGE, n_state), BF16),
-            V((batch, 8, length), F32),
+            V((batch, length), jnp.int32),
             V((batch, taps - 1, length, cw), F32),
             V((batch, length, channels), BF16),
             V((batch, length, n_state), BF16),
@@ -516,20 +587,24 @@
             V((steps, n_state, cw), BF16),
             V((units, n_state, cw), BF16),
             V((batch, length, channels), F32),
+            V((batch, length, channels), F32),
             V((length, channels), BF16),
             V((batch * others * pieces, length, piece), BF16),
             V((batch * others * pieces, length, piece), BF16),
             V((batch * pieces, length, piece), F32),
             V((batch, 8, length), F32),
             V((batch * others, 8, length), F32),
+            dma((batch,)),
             dma,
             dma((n_mp * pieces,)),
-            dma((4,)),
-            dma((4,)),
+            dma,
+            dma,
+            dma((batch, 3)),
+            dma((batch, 3)),
             dma((steps,)),
             dma((steps,)),
-            dma,
-            dma,
+            dma((batch,)),
+            dma((batch,)),
             dma((steps,)),
             dma((steps,)),
             dma((steps,)),
@@ -548,14 +623,14 @@
         z_gate,
         b_input,
         c_input,
-        dt_raw,
-        docs,
+        jnp.swapaxes(dt_raw, 1, 2),
+        doc_ids,
         conv_x,
         conv_b,
         conv_c,
         dt_bias[None, :],
         decay_rate[None, :],
-        norm_gain[None, :],
+        norm_gain.reshape(channels // cw, cw),
         weights,
     )
 

time: 93.5 us -> 98.9 us (1.058)
  the two profiles are of different devices: /device:TPU:27 before, /device:TPU:10 now
where the time goes in v2:
time: 98.9 us; the launch traced here: 98.7 us
  Pallas kernels  96.3 us (97%)
  local copies, waits for them, and re-layouts  2.46 us (2%)
    pallas_call x1, Pallas kernels, body(): pl.pallas_call(functools.partial(kernel, dims), out_shape=jax.ShapeDtypeS...  96.3 us
    unnamed x1, local copies, waits for them, and re-layouts  2.46 us

profile of v2, /device:TPU:10, one launch (start us, length us, event | category | flops | bytes accessed | tf_op | source)
XLA Modules:
  0.0 98.7 jit_solution(16081421713360398086)
XLA Ops:
  0.0 96.3 %mixer.1 = bf16[2,256,1280]{2,1,0:T(8,128)(2,1)} custom-call(bf16[2,256,2560]{2,1,0:T(8,128)(2,1)} %x_hbm.1, bf16[2,256,2560]{2,1,0:T(8,128)(2,1)} %z_hbm.1, bf16[2,256,128]{2,1,0:T(8,128)(2,1)} %b_ref.1, bf16[2,256,128]{2,1,0:T(8,128)(2,1)} %c_ref.1, f32[2,40,256]{2,1,0:T(8,128)} %bitcast.4, s32[2,256]{1,0:T(2,128)} %doc_ref.1, bf16[4,2560]{1,0:T(4,128)(2,1)} %wx_ref.1, ...), custom_call_target="tpu_custom_call" | custom-call | tf_op jit(solution)/shard_map/mixer/pallas_call | solution.py:558
  96.3 2.5 %copy.15 = bf16[2,256,1280]{2,1,0:T(8,128)(2,1)} copy(bf16[2,256,1280]{2,1,0:T(8,128)(2,1)} %mixer.1) | data formatting | bytes 2621440

commit v3 on v2

--- a/solution.py
+++ b/solution.py
@@ -105,6 +105,7 @@
     units = batch * chunks
     steps = units // 2
     pieces = width // piece
+    tiles = 4 if chunks % 4 == 0 else 2
     n_seq = lax.axis_size("seq")
     me = lax.axis_index("seq")
     my = lax.axis_index("mp")
@@ -282,7 +283,7 @@
             s_ref.at[u], r_ref.at[u // 2], s_send.at[u // 2], s_recv.at[u // 2], seq=sibling
         )
 
-    def front(u, _):
+    def front_unit(u):
         b, c, where = place(u)
         sames = [same_ref[b, lag] for lag in range(wx_ref.shape[0] - 1)]
         x_conv = conv(x_ref[b, :, where], hx_ref[b, :, where], wx_ref[:, where], sames)
@@ -294,10 +295,11 @@
         gate = expand(turned(entry_ref[b, length - 8 : length, :], c))
         g_ref[u] = jnp.broadcast_to(gate[7:8], (8, cw))
 
-        @pl.when(lax.rem(u, 2) != core)
-        def _():
-            s_copy(u).start()
-
+    def front(group, _):
+        for k in range(tiles):
+            front_unit(group * tiles + k)
+        for k in range(0, tiles, 2):
+            s_copy(group * tiles + k + 1 - core).start()
         return 0
 
     bounds = [((b * chunks + 1) // 2, ((b + 1) * chunks + 1) // 2) for b in range(batch)]
@@ -314,7 +316,7 @@
             for every in range(batch):
                 prepare(every)
         lower, upper = bounds[b]
-        lax.fori_loop(2 * lower, 2 * upper, front, 0)
+        lax.fori_loop(2 * lower // tiles, 2 * upper // tiles, front, 0)
         g_copy(b).start()
 
     ahead = lax.rem(me + 2, n_seq)
@@ -326,27 +328,41 @@
         u = 2 * i + owner
         return remote(t_ref.at[i], en_ref.at[u], t_send.at[i], t_recv.at[i], seq=sibling)
 
-    def inner_unit(u, _):
+    def inner_unit(u):
         b, c, where = place(u)
         turned_logs = turned(col_ref[b], c)
-        scores = score_ref[b]
+        cut = length // 2
         for tile in range(cw // LANES):
             lanes = pl.ds(pl.multiple_of(c * cw + tile * LANES, LANES), LANES)
             xs = xc_ref[b, :, lanes]
-            total = None
+            upper_rows, lower_rows = None, None
             for more in range(per_tile):
                 head = tile * per_tile + more
                 column = turned_logs[:, head : head + 1]
                 row = row_ref[b, pl.ds(c * per_chunk + head, 1), :]
-                mixing = scores * jnp.exp2(jnp.minimum(column - row, CAP))
-                one = jnp.dot(mixing.astype(BF16), xs, preferred_element_type=F32)
-                total = one if more == 0 else jnp.where(lane_ids < more * head_dim, total, one)
+                spread = jnp.exp2(jnp.minimum(column[:cut] - row[:, :cut], CAP))
+                mixing = (score_ref[b, :cut, :cut] * spread).astype(BF16)
+                one = jnp.dot(mixing, xs[:cut], preferred_element_type=F32)
+                spread = jnp.exp2(jnp.minimum(column[cut:] - row, CAP))
+                mixing = (score_ref[b, cut:, :] * spread).astype(BF16)
+                two = jnp.dot(mixing, xs, preferred_element_type=F32)
+                if more == 0:
+                    upper_rows, lower_rows = one, two
+                else:
+                    chosen = lane_ids[:cut] < more * head_dim
+                    upper_rows = jnp.where(chosen, upper_rows, one)
+                    lower_rows = jnp.where(chosen, lower_rows, two)
+            total = jnp.concatenate([upper_rows, lower_rows], axis=0)
             opened = silu(z_ref[b, :, lanes].astype(F32))
             inner_ref[b, :, lanes] = total * opened
             factor_ref[b, :, lanes] = expand(turned(entry_ref[b], c)) * opened
+
+    def inner(group, _):
+        for k in range(tiles):
+            inner_unit(group * tiles + k)
         return 0
 
-    def chain(i, _):
+    def chain(i, _, fill=False):
         u = 2 * i + core
         s_copy(2 * i).wait_recv()
         mine, theirs = s_ref[u].astype(F32), r_ref[i].astype(F32)
@@ -372,6 +388,9 @@
         t_ref[i] = jnp.where(first, middle, entering).astype(BF16)
         t_copy(i, core).start()
         en_ref[u] = jnp.where(first, entering, middle).astype(BF16)
+        if fill:
+            inner_unit(2 * i)
+            inner_unit(2 * i + 1)
         return 0
 
     def t_wait(i, _):
@@ -402,17 +421,20 @@
         )
 
     def tail(b):
-        def gate_unit(c, squares):
-            where = pl.ds(pl.multiple_of(c * cw, cw), cw)
-            outer = jnp.dot(cc_ref[b], en_ref[b * chunks + c], preferred_element_type=F32)
-            gated = inner_ref[b, :, where] + factor_ref[b, :, where] * outer
-            gn_ref[:, where] = (gated * gain_ref[pl.ds(c, 1), :]).astype(BF16)
-            square = gated * gated
-            for tile in range(cw // LANES):
-                squares = squares + square[:, tile * LANES : (tile + 1) * LANES]
+        span = 4 if chunks % 4 == 0 else 1
+
+        def gate_units(group, squares):
+            for k in range(span):
+                c = group * span + k
+                where = pl.ds(pl.multiple_of(c * cw, cw), cw)
+                outer = jnp.dot(cc_ref[b], en_ref[b * chunks + c], preferred_element_type=F32)
+                gated = inner_ref[b, :, where] + factor_ref[b, :, where] * outer
+                gn_ref[:, where] = (gated * gain_ref[pl.ds(c, 1), :]).astype(BF16)
+                squares = squares + gated * gated
             return squares
 
-        squares = lax.fori_loop(0, chunks, gate_unit, jnp.zeros((length, LANES), F32))
+        squares = jnp.zeros((length, LANES), F32)
+        squares = lax.fori_loop(0, chunks // span, gate_units, squares)
         sq_ref[b] = jnp.broadcast_to(jnp.sum(squares.T, axis=0, keepdims=True), (8, length))
         for r in range(1, n_mp):
 
@@ -447,37 +469,43 @@
                 value = value + q_ref[p_slot(b, r, p)].astype(F32)
             out_ref[b, :, p * piece : (p + 1) * piece] = (value * scale).astype(BF16)
 
-    def inners():
-        z_copy.wait()
-        lax.fori_loop(0, units, inner_unit, 0)
-
-    def chains(b):
+    def inners(lower, upper):
+        lax.fori_loop(lower, upper, inner, 0)
+
+    def chains(b, fill):
         lower, upper = bounds[b]
         g_copy(b).wait_recv()
-        lax.fori_loop(lower, upper, chain, 0)
+        lax.fori_loop(lower, upper, functools.partial(chain, fill=fill), 0)
 
     def returns(b):
         lower, upper = bounds[b]
         lax.fori_loop(lower, upper, t_wait, 0)
 
     late = me >= n_seq // 2
+    last = me >= 3 * n_seq // 4
+    half, whole = 2 * bounds[0][1] // tiles, units // tiles
+    ready = jnp.where(last, whole, jnp.where(late, half, 0))
     fronts(0)
 
     @pl.when(late)
     def _():
         for b in range(1, batch):
             fronts(b)
-        inners()
-
-    chains(0)
+
+    z_copy.wait()
+
+    @pl.when(late)
+    def _():
+        inners(0, ready)
+        chains(0, False)
 
     @pl.when(jnp.logical_not(late))
     def _():
+        chains(0, True)
         for b in range(1, batch):
             fronts(b)
         for b in range(1, batch):
-            chains(b)
-        inners()
+            chains(b, True)
 
     lax.fori_loop(0, n_mp * pieces, lambda k, _: (w_copy(k).wait(), 0)[1], 0)
     for b in range(batch):
@@ -485,7 +513,8 @@
 
             @pl.when(late)
             def _(b=b):
-                chains(b)
+                chains(b, False)
+                inners(ready, whole)
 
         returns(b)
         tail(b)

time: 98.9 us -> 79.4 us (0.80)
  Pallas kernels: 96.3 us -> 76.7 us
    pallas_call x1, Pallas kernels: 96.3 us -> 76.7 us  [body(): pl.pallas_call(functools.partial(kernel, dims), out_shape=jax.ShapeDtypeS...]
where the time goes in v3:
time: 79.4 us; the launch traced here: 79.2 us
  Pallas kernels  76.7 us (97%)
  local copies, waits for them, and re-layouts  2.46 us (3%)
    pallas_call x1, Pallas kernels, body(): pl.pallas_call(functools.partial(kernel, dims), out_shape=jax.ShapeDtypeS...  76.7 us
    unnamed x1, local copies, waits for them, and re-layouts  2.46 us

profile of v3, /device:TPU:10, one launch (start us, length us, event | category | flops | bytes accessed | tf_op | source)
XLA Modules:
  0.0 79.2 jit_solution(2445884967615429249)
XLA Ops:
  0.0 76.7 %mixer.1 = bf16[2,256,1280]{2,1,0:T(8,128)(2,1)} custom-call(bf16[2,256,2560]{2,1,0:T(8,128)(2,1)} %x_hbm.1, bf16[2,256,2560]{2,1,0:T(8,128)(2,1)} %z_hbm.1, bf16[2,256,128]{2,1,0:T(8,128)(2,1)} %b_ref.1, bf16[2,256,128]{2,1,0:T(8,128)(2,1)} %c_ref.1, f32[2,40,256]{2,1,0:T(8,128)} %bitcast.4, s32[2,256]{1,0:T(2,128)} %doc_ref.1, bf16[4,2560]{1,0:T(4,128)(2,1)} %wx_ref.1, ...), custom_call_target="tpu_custom_call" | custom-call | tf_op jit(solution)/shard_map/mixer/pallas_call | solution.py:587
  76.7 2.5 %copy.15 = bf16[2,256,1280]{2,1,0:T(8,128)(2,1)} copy(bf16[2,256,1280]{2,1,0:T(8,128)(2,1)} %mixer.1) | data formatting | bytes 2621440

commit v4 on v3

--- a/solution.py
+++ b/solution.py
@@ -362,7 +362,7 @@
             inner_unit(group * tiles + k)
         return 0
 
-    def chain(i, _, fill=False):
+    def chain(i, _, fill=None):
         u = 2 * i + core
         s_copy(2 * i).wait_recv()
         mine, theirs = s_ref[u].astype(F32), r_ref[i].astype(F32)
@@ -388,9 +388,13 @@
         t_ref[i] = jnp.where(first, middle, entering).astype(BF16)
         t_copy(i, core).start()
         en_ref[u] = jnp.where(first, entering, middle).astype(BF16)
-        if fill:
-            inner_unit(2 * i)
-            inner_unit(2 * i + 1)
+        if fill is not None:
+
+            @pl.when(2 * i >= fill)
+            def _():
+                inner_unit(2 * i)
+                inner_unit(2 * i + 1)
+
         return 0
 
     def t_wait(i, _):
@@ -484,7 +488,8 @@
     late = me >= n_seq // 2
     last = me >= 3 * n_seq // 4
     half, whole = 2 * bounds[0][1] // tiles, units // tiles
-    ready = jnp.where(last, whole, jnp.where(late, half, 0))
+    more = half + (whole - half) // 2
+    ready = jnp.where(last, more, jnp.where(late, half, 0))
     fronts(0)
 
     @pl.when(late)
@@ -497,15 +502,15 @@
     @pl.when(late)
     def _():
         inners(0, ready)
-        chains(0, False)
+        chains(0, None)
 
     @pl.when(jnp.logical_not(late))
     def _():
-        chains(0, True)
+        chains(0, 0)
         for b in range(1, batch):
             fronts(b)
         for b in range(1, batch):
-            chains(b, True)
+            chains(b, 0)
 
     lax.fori_loop(0, n_mp * pieces, lambda k, _: (w_copy(k).wait(), 0)[1], 0)
     for b in range(batch):
@@ -513,8 +518,7 @@
 
             @pl.when(late)
             def _(b=b):
-                chains(b, False)
-                inners(ready, whole)
+                chains(b, ready * tiles)
 
         returns(b)
         tail(b)

time: 79.4 us -> 79.6 us (level)
  no operation moved by 1% of the time
where the time goes in v4:
time: 79.6 us; the launch traced here: 79.5 us
  Pallas kernels  77 us (97%)
  local copies, waits for them, and re-layouts  2.46 us (3%)
    pallas_call x1, Pallas kernels, body(): pl.pallas_call(functools.partial(kernel, dims), out_shape=jax.ShapeDtypeS...  77 us
    unnamed x1, local copies, waits for them, and re-layouts  2.46 us

profile of v4, /device:TPU:10, one launch (start us, length us, event | category | flops | bytes accessed | tf_op | source)
XLA Modules:
  0.0 79.5 jit_solution(7603079664051979841)
XLA Ops:
  0.0 77.0 %mixer.1 = bf16[2,256,1280]{2,1,0:T(8,128)(2,1)} custom-call(bf16[2,256,2560]{2,1,0:T(8,128)(2,1)} %x_hbm.1, bf16[2,256,2560]{2,1,0:T(8,128)(2,1)} %z_hbm.1, bf16[2,256,128]{2,1,0:T(8,128)(2,1)} %b_ref.1, bf16[2,256,128]{2,1,0:T(8,128)(2,1)} %c_ref.1, f32[2,40,256]{2,1,0:T(8,128)} %bitcast.4, s32[2,256]{1,0:T(2,128)} %doc_ref.1, bf16[4,2560]{1,0:T(4,128)(2,1)} %wx_ref.1, ...), custom_call_target="tpu_custom_call" | custom-call | tf_op jit(solution)/shard_map/mixer/pallas_call | solution.py:591
  77.0 2.5 %copy.15 = bf16[2,256,1280]{2,1,0:T(8,128)(2,1)} copy(bf16[2,256,1280]{2,1,0:T(8,128)(2,1)} %mixer.1) | data formatting | bytes 2621440
